TPU v7x, 32 devices: a whole 2x2x4 slice. The times are simulated.
32 devices in a mesh: row: 4 (over z), col: 8 (over y, x, core).
Axes of the slice: x: 2, y: 2, z: 4, core: 2. Of those that a mesh axis runs over, the one named last changes fastest.
Arguments:
- rho_real: float32 [4096, 4096], P('row', 'col'), may hold values from -2.5 to 4, as said below
- rho_imag: float32 [4096, 4096], P('row', 'col'), may hold values from -2.5 to 2.5, as said below
- hamiltonian: bfloat16 [4096, 4096], P('row', 'col'), may hold values from -1 to 1
- amplitudes: float32 [8, 4096], replicated, may hold values from 0.15 to 0.6
- offsets: int32 [8], replicated, may hold values from -16 to 16
- active_jumps: int32 [1], replicated, may hold values from 4 to 8
Outputs:
- rho_next_real: float32 [4096, 4096], P('row', 'col')
- rho_next_imag: float32 [4096, 4096], P('row', 'col')
Inputs may be any that keep to these rules, and one draw needn't show every extreme that they name: `rho_real`: symmetric, with every diagonal entry 0.5 or more. `rho_imag`: antisymmetric.
All inputs are finite; a program needn't handle non-finite values.
Results may differ from a plain program's by a relative error of at most 0.001.
Values may be sent and summed in bfloat16 or wider, within the bound.
A program may use at most 192 MiB of HBM per device.

v0:
```python
import jax
import jax.numpy as jnp
from jax import lax
from jax.sharding import PartitionSpec as P

OMAX = 16
step_size = 0.25


def extended(cells, sides, width):
    for axis, dim in sides:
        count = lax.axis_size(axis)
        ends = count - 1
        head = lax.slice_in_dim(cells, 0, width, axis=dim)
        tail = lax.slice_in_dim(cells, cells.shape[dim] - width, cells.shape[dim], axis=dim)
        cells = jnp.concatenate(
            [
                lax.ppermute(tail, axis, [(i, (i + 1) % count) for i in range(ends)]),
                cells,
                lax.ppermute(head, axis, [((i + 1) % count, i) for i in range(ends)]),
            ],
            axis=dim,
        )
    return cells


def dissipate(matrix, padded, amplitudes, offsets, active, row_first, col_first):
    height = matrix.shape[1]
    breadth = matrix.shape[2]
    levels = amplitudes.shape[1]
    margin = (padded.shape[1] - height) // 2
    positions = jnp.arange(levels, dtype=jnp.int32)
    summed = jnp.zeros(matrix.shape, matrix.dtype)
    for jump_slot in range(amplitudes.shape[0]):
        offset = offsets[jump_slot]
        inside = (positions + offset >= 0) & (positions + offset < levels)
        strength = jnp.where(inside, amplitudes[jump_slot], 0.0)
        outflow = jnp.pad(strength * strength, (margin, margin))
        outflow = lax.dynamic_slice_in_dim(outflow, margin - offset, levels)
        row_strength = lax.dynamic_slice_in_dim(strength, row_first, height)
        col_strength = lax.dynamic_slice_in_dim(strength, col_first, breadth)
        row_outflow = lax.dynamic_slice_in_dim(outflow, row_first, height)
        col_outflow = lax.dynamic_slice_in_dim(outflow, col_first, breadth)
        corner = margin + offset
        shifted = lax.dynamic_slice(padded, (jnp.int32(0), corner, corner), (2, height, breadth))
        contribution = (
            row_strength[:, None] * col_strength[None, :] * shifted
            - 0.5 * (row_outflow[:, None] + col_outflow[None, :]) * matrix
        )
        summed = summed + jnp.where(jump_slot < active, contribution, 0.0)
    return summed


def diagonal_sum(matrix, row_first, col_first):
    row_index = lax.broadcasted_iota(jnp.int32, matrix.shape, 0) + row_first
    col_index = lax.broadcasted_iota(jnp.int32, matrix.shape, 1) + col_first
    return jnp.sum(jnp.where(row_index == col_index, matrix, 0.0))


def local(rho_real, rho_imag, hamiltonian, amplitudes, offsets, active_jumps):
    height, breadth = rho_real.shape
    levels = amplitudes.shape[1]
    row_first = lax.axis_index("row") * height
    col_first = lax.axis_index("col") * breadth
    active = active_jumps[0]
    ham_columns = lax.all_gather(hamiltonian, "row", axis=0, tiled=True)
    start_trace = lax.psum(diagonal_sum(rho_real, row_first, col_first), ("row", "col"))

    def drift(real_part, imag_part):
        real_low = real_part.astype(jnp.bfloat16)
        imag_low = imag_part.astype(jnp.bfloat16)
        row_panel = lax.all_gather(hamiltonian, "col", axis=1, tiled=True)
        pieces = (
            lax.all_gather(real_low, "row", axis=0, tiled=True),
            lax.all_gather(imag_low, "row", axis=0, tiled=True),
        )
        strip = row_panel
        left_real = jnp.dot(strip, pieces[0], preferred_element_type=jnp.float32)
        left_imag = jnp.dot(strip, pieces[1], preferred_element_type=jnp.float32)
        pieces = (
            lax.all_gather(real_low, "col", axis=1, tiled=True),
            lax.all_gather(imag_low, "col", axis=1, tiled=True),
        )
        strip = ham_columns
        right_real = jnp.dot(pieces[0], strip, preferred_element_type=jnp.float32)
        right_imag = jnp.dot(pieces[1], strip, preferred_element_type=jnp.float32)
        matrix = jnp.stack([real_part, imag_part])
        padded = extended(matrix.astype(jnp.bfloat16), (("row", 1), ("col", 2)), OMAX).astype(
            matrix.dtype
        )
        loss = dissipate(matrix, padded, amplitudes, offsets, active, row_first, col_first)
        return (left_imag - right_imag + loss[0], right_real - left_real + loss[1])

    first_real, first_imag = drift(rho_real, rho_imag)
    middle_real = rho_real + step_size * first_real
    middle_imag = rho_imag + step_size * first_imag
    rescale = levels / start_trace
    middle_real = middle_real * rescale
    middle_imag = middle_imag * rescale
    second_real, second_imag = drift(middle_real, middle_imag)
    updated_real = rho_real + 0.5 * step_size * (first_real + second_real)
    updated_imag = rho_imag + 0.5 * step_size * (first_imag + second_imag)
    rescale = levels / start_trace
    return (updated_real * rescale, updated_imag * rescale)


def solution(mesh):
    in_specs = (P("row", "col"), P("row", "col"), P("row", "col"), P(), P(), P())
    out_specs = (P("row", "col"), P("row", "col"))
    return jax.shard_map(local, mesh=mesh, in_specs=in_specs, out_specs=out_specs, check_vma=False)
```

profile of v0, /device:TPU:0, one launch (start us, length us, event | category | flops | bytes accessed | tf_op | source)
XLA Modules:
  0.0 739.0 jit_solution(2727342368948847065)
XLA Ops:
  7.2 2.7 convert_element_type.41
  10.0 0.7 all-gather.11.cloned.1.call-update
  10.8 0.7 all-gather.17.cloned.1.call-update
  11.5 0.5 all-gather.15.cloned.1.call-update
  12.1 2.0 fusion.1
  14.1 1.3 copy-done.4
  15.4 4.9 collective-permute-start
  20.4 1.3 collective-permute-start.1
  21.7 0.7 fusion.69
  32.6 0.6 fusion.62
  33.3 0.6 fusion.64
  34.1 0.6 fusion.58
  34.8 0.7 fusion.60
  35.6 0.6 fusion.54
  36.3 0.7 fusion.56
  37.6 0.6 fusion.52
  38.3 0.6 fusion.50
  39.6 2.4 add_multiply_fusion.2
  41.9 2.3 add_multiply_fusion.4
  44.3 2.4 add_multiply_fusion.6
  46.7 2.3 add_multiply_fusion.8
  49.0 2.4 broadcast_multiply_fusion
  51.3 2.4 broadcast_multiply_fusion.2
  53.7 2.5 broadcast_multiply_fusion.4
  56.2 1.3 select_reduce_fusion
  58.1 1.5 collective-permute-start.2
  59.8 1.3 collective-permute-start.3
  61.1 2.4 broadcast_multiply_fusion.6
  63.5 47.8 %psum.7 = f32[]{:T(128)} all-reduce(f32[]{:T(128)} %select_reduce_fusion), channel_id=1, replica_groups=mesh['row'=4,'col'=8] {'row','col'}, use_global_device_ids=true, to_apply=%region_1.2 | all-reduce | flops 1 | bytes 8 | tf_op jit(solution)/shard_map/psum | solution.py:67
  127.8 0.3 copy.12
  128.1 0.3 copy.13
  128.4 5.1 maximum_convert_fusion
  133.5 28.7 %select_add_fusion.1 = f32[2,1024,512]{2,1,0:T(8,128)} fusion(f32[2,1056,544]{2,1,0:T(8,128)} %maximum_convert_fusion, s32[]{:T(128)S(6)} %select_n.358, s32[]{:T(128)S(6)} %select_n.359, s32[]{:T(128)S(6)} %select_n.351, s32[]{:T(128)S(6)} %select_n.352, s32[]{:T(128)S(6)} %select_n.344, s32[]{:T(128)S(6)} %select_n.345, s32[]{:T(128)S(6)} %select_n.337, ...), kind=kLoop, calls=%fused_computation.3 | loop fusion | flops 41943040 | bytes 75497544 | tf_op jit(solution)/shard_map/add | solution.py:50
  162.2 10.7 %fusion.70 = f32[1024,512]{1,0:T(8,128)} fusion(bf16[1024,4096]{1,0:T(8,128)(2,1)} %all-gather.11.cloned.1.call-done, bf16[4096,512]{1,0:T(8,128)(2,1)} %all-gather.13.cloned.1.call-done), kind=kOutput, calls=%fused_computation.125 | convolution fusion | flops 4294967296 | bytes 14680064 | tf_op jit(solution)/shard_map/dot_general | solution.py:79
  172.9 61.1 %all-gather.17.cloned.1.call-done = bf16[4096,512]{1,0:T(8,128)(2,1)} async-done(((bf16[1024,512]{1,0:T(8,128)(2,1)}), bf16[4096,512]{1,0:T(8,128)(2,1)}) %all-gather.17.cloned.1.call-update) | async-done | bytes 4194320 | tf_op jit(solution)/shard_map/all_gather | solution.py:66
  234.0 56.1 %all-gather.15.cloned.1.call-done = bf16[1024,4096]{1,0:T(8,128)(2,1)} async-done(((bf16[1024,512]{1,0:T(8,128)(2,1)}), bf16[1024,4096]{1,0:T(8,128)(2,1)}) %all-gather.15.cloned.1.call-update) | async-done | bytes 8388624 | tf_op jit(solution)/shard_map/all_gather | solution.py:82
  290.2 10.5 %fusion.13 = f32[1024,512]{1,0:T(8,128)S(1)} fusion(f32[2,1024,512]{2,1,0:T(8,128)} %select_add_fusion.1, f32[1024,512]{1,0:T(8,128)} %fusion.70, bf16[1024,4096]{1,0:T(8,128)(2,1)} %all-gather.15.cloned.1.call-done, bf16[4096,512]{1,0:T(8,128)(2,1)} %all-gather.17.cloned.1.call-done), kind=kOutput, calls=%fused_computation.23 | convolution fusion | flops 4296015872 | bytes 18874368 | tf_op jit(solution)/shard_map/dot_general | solution.py:86
  300.6 2.7 fusion.16
  303.4 0.5 all-gather.21.cloned.1.call-update
  304.0 0.7 all-gather.27.cloned.1.call-update
  304.7 0.7 all-gather.29.cloned.1.call-update
  305.7 53.7 %all-gather.19.cloned.1.call-done = bf16[1024,4096]{1,0:T(8,128)(2,1)} async-done(((bf16[1024,512]{1,0:T(8,128)(2,1)}), bf16[1024,4096]{1,0:T(8,128)(2,1)}) %all-gather.19.cloned.1.call-update) | async-done | bytes 8388624 | tf_op jit(solution)/shard_map/all_gather | solution.py:81
  359.4 10.5 %fusion.71 = f32[1024,512]{1,0:T(8,128)} fusion(bf16[1024,4096]{1,0:T(8,128)(2,1)} %all-gather.19.cloned.1.call-done, bf16[4096,512]{1,0:T(8,128)(2,1)} %all-gather.17.cloned.1.call-done), kind=kOutput, calls=%fused_computation.126 | convolution fusion | flops 4294967296 | bytes 14680064 | tf_op jit(solution)/shard_map/dot_general | solution.py:85
  369.8 71.7 %all-gather.21.cloned.1.call-done = bf16[4096,512]{1,0:T(8,128)(2,1)} async-done(((bf16[1024,512]{1,0:T(8,128)(2,1)}), bf16[4096,512]{1,0:T(8,128)(2,1)}) %all-gather.21.cloned.1.call-update) | async-done | bytes 4194320 | tf_op jit(solution)/shard_map/all_gather | solution.py:74
  441.6 10.3 %fusion.12 = f32[1024,512]{1,0:T(8,128)S(1)} fusion(f32[2,1024,512]{2,1,0:T(8,128)} %select_add_fusion.1, f32[1024,512]{1,0:T(8,128)} %fusion.71, bf16[1024,4096]{1,0:T(8,128)(2,1)} %all-gather.11.cloned.1.call-done, bf16[4096,512]{1,0:T(8,128)(2,1)} %all-gather.21.cloned.1.call-done), kind=kOutput, calls=%fused_computation.21 | convolution fusion | flops 4296015872 | bytes 18874368 | tf_op jit(solution)/shard_map/dot_general | solution.py:78
  451.9 2.5 fusion.15
  454.5 2.6 fusion
  457.1 1.3 copy-done.6
  458.4 1.3 collective-permute-start.4
  459.7 1.3 collective-permute-start.5
  461.3 4.3 collective-permute-done.5
  465.6 1.5 pad_maximum_fusion.4
  467.3 1.3 collective-permute-start.6
  468.8 1.3 collective-permute-start.7
  470.1 27.8 %all-gather.27.cloned.1.call-done = bf16[1024,4096]{1,0:T(8,128)(2,1)} async-done(((bf16[1024,512]{1,0:T(8,128)(2,1)}), bf16[1024,4096]{1,0:T(8,128)(2,1)}) %all-gather.27.cloned.1.call-update) | async-done | bytes 8388624 | tf_op jit(solution)/shard_map/all_gather | solution.py:81
  497.9 10.4 %fusion.73 = f32[1024,512]{1,0:T(8,128)} fusion(bf16[1024,4096]{1,0:T(8,128)(2,1)} %all-gather.27.cloned.1.call-done, bf16[4096,512]{1,0:T(8,128)(2,1)} %all-gather.17.cloned.1.call-done), kind=kOutput, calls=%fused_computation.128 | convolution fusion | flops 4294967296 | bytes 14680064 | tf_op jit(solution)/shard_map/dot_general | solution.py:85
  508.9 5.4 maximum_convert_fusion.1
  514.3 29.5 %select_add_fusion = f32[2,1024,512]{2,1,0:T(8,128)} fusion(f32[2,1056,544]{2,1,0:T(8,128)} %maximum_convert_fusion.1, s32[]{:T(128)S(6)} %select_n.358, s32[]{:T(128)S(6)} %select_n.359, s32[]{:T(128)S(6)} %select_n.351, s32[]{:T(128)S(6)} %select_n.352, s32[]{:T(128)S(6)} %select_n.344, s32[]{:T(128)S(6)} %select_n.345, s32[]{:T(128)S(6)} %select_n.337, ...), kind=kLoop, calls=%fused_computation.2 | loop fusion | flops 41943040 | bytes 75497544 | tf_op jit(solution)/shard_map/add | solution.py:50
  543.7 37.2 %all-gather.29.cloned.1.call-done = bf16[4096,512]{1,0:T(8,128)(2,1)} async-done(((bf16[1024,512]{1,0:T(8,128)(2,1)}), bf16[4096,512]{1,0:T(8,128)(2,1)}) %all-gather.29.cloned.1.call-update) | async-done | bytes 4194320 | tf_op jit(solution)/shard_map/all_gather | solution.py:74
  580.9 12.5 %fusion.6 = f32[1024,512]{1,0:T(8,128)} fusion(f32[1024,512]{1,0:T(8,128)S(1)} %copy-done, f32[1024,512]{1,0:T(8,128)} %copy-done.8, f32[2,1024,512]{2,1,0:T(8,128)} %select_add_fusion, f32[1024,512]{1,0:T(8,128)} %fusion.73, bf16[1024,4096]{1,0:T(8,128)(2,1)} %all-gather.11.cloned.1.call-done, bf16[4096,512]{1,0:T(8,128)(2,1)} %all-gather.29.cloned.1.call-done, ...), kind=kOutput, calls=%fused_computation.13 | convolution fusion | flops 4298113024 | bytes 23068676 | tf_op jit(solution)/shard_map/dot_general | solution.py:78
  593.4 43.8 %all-gather.25.cloned.1.call-done = bf16[1024,4096]{1,0:T(8,128)(2,1)} async-done(((bf16[1024,512]{1,0:T(8,128)(2,1)}), bf16[1024,4096]{1,0:T(8,128)(2,1)}) %all-gather.25.cloned.1.call-update) | async-done | bytes 8388624 | tf_op jit(solution)/shard_map/all_gather | solution.py:82
  637.2 10.5 %fusion.72 = f32[1024,512]{1,0:T(8,128)} fusion(bf16[1024,4096]{1,0:T(8,128)(2,1)} %all-gather.25.cloned.1.call-done, bf16[4096,512]{1,0:T(8,128)(2,1)} %all-gather.17.cloned.1.call-done), kind=kOutput, calls=%fused_computation.127 | convolution fusion | flops 4294967296 | bytes 14680064 | tf_op jit(solution)/shard_map/dot_general | solution.py:86
  647.7 71.7 %all-gather.23.cloned.1.call-done = bf16[4096,512]{1,0:T(8,128)(2,1)} async-done(((bf16[1024,512]{1,0:T(8,128)(2,1)}), bf16[4096,512]{1,0:T(8,128)(2,1)}) %all-gather.23.cloned.1.call-update) | async-done | bytes 4194320 | tf_op jit(solution)/shard_map/all_gather | solution.py:75
  719.4 12.5 %fusion.11 = f32[1024,512]{1,0:T(8,128)} fusion(f32[1024,512]{1,0:T(8,128)S(1)} %copy-done.3, f32[1024,512]{1,0:T(8,128)} %copy-done.7, f32[2,1024,512]{2,1,0:T(8,128)} %select_add_fusion, f32[1024,512]{1,0:T(8,128)} %fusion.72, bf16[1024,4096]{1,0:T(8,128)(2,1)} %all-gather.11.cloned.1.call-done, bf16[4096,512]{1,0:T(8,128)(2,1)} %all-gather.23.cloned.1.call-done, ...), kind=kOutput, calls=%fused_computation.19 | convolution fusion | flops 4298113024 | bytes 23068676 | tf_op jit(solution)/shard_map/dot_general | solution.py:79
  (87 shorter events, 4.7 us)
Async XLA Ops:
  7.2 155.0 %all-gather.13.cloned.1.call-start = ((), (), s32[]{:S(2)}) async-start(), calls=%async_computation.1 | async-start | bytes 5242880 | tf_op jit(solution)/shard_map/all_gather | solution.py:75
  9.9 2.1 copy-start
  10.0 152.2 %all-gather.11.cloned.1.call-start = ((), (), s32[]{:S(2)}) async-start(), calls=%async_computation | async-start | bytes 9437184 | tf_op jit(solution)/shard_map/all_gather | solution.py:72
  10.7 223.3 %all-gather.17.cloned.1.call-start = ((), (), s32[]{:S(2)}) async-start(), calls=%async_computation.3 | async-start | bytes 5242880 | tf_op jit(solution)/shard_map/all_gather | solution.py:66
  11.4 278.7 %all-gather.15.cloned.1.call-start = ((), (), s32[]{:S(2)}) async-start(), calls=%async_computation.2 | async-start | bytes 9437184 | tf_op jit(solution)/shard_map/all_gather | solution.py:82
  12.0 347.3 %all-gather.19.cloned.1.call-start = ((), (), s32[]{:S(2)}) async-start(), calls=%async_computation.4 | async-start | bytes 9437184 | tf_op jit(solution)/shard_map/all_gather | solution.py:81
  12.1 9.6 %copy-start.10 = (s32[8]{0:T(128)S(1)}, s32[8]{0:T(128)}, u32[]{:S(2)}) copy-start(s32[8]{0:T(128)} %param.10) | copy-start | bytes 100
  12.1 20.4 %copy-start.9 = (f32[8,4096]{1,0:T(8,128)S(1)}, f32[8,4096]{1,0:T(8,128)}, u32[]{:S(2)}) copy-start(f32[8,4096]{1,0:T(8,128)} %param.9) | copy-start | bytes 393220
  14.1 1.3 copy-start.4
  15.4 42.2 %collective-permute-start = (bf16[2,16,512]{2,1,0:T(8,128)(2,1)S(1)}, bf16[2,16,512]{2,1,0:T(8,128)(2,1)S(1)}, u32[]{:S(2)}, u32[]{:S(2)}) collective-permute-start(bf16[2,16,512]{2,1,0:T(8,128)(2,1)S(1)} %get-tuple-element.29), channel_id=1, source_target_pairs={{0,8},{8,16},{16,24},{1,9},{9,17},{17,25},{2,10},{10,18},{18,26},{... | collective-permute-start | bytes 98312 | tf_op jit(solution)/shard_map/ppermute | solution.py:18
  20.4 37.3 %collective-permute-start.1 = (bf16[2,16,512]{2,1,0:T(8,128)(2,1)S(1)}, bf16[2,16,512]{2,1,0:T(8,128)(2,1)S(1)}, u32[]{:S(2)}, u32[]{:S(2)}) collective-permute-start(bf16[2,16,512]{2,1,0:T(8,128)(2,1)S(1)} %get-tuple-element.30), channel_id=1, source_target_pairs={{8,0},{16,8},{24,16},{9,1},{17,9},{25,17},{10,2},{18,10},{26,18},{... | collective-permute-start | bytes 98312 | tf_op jit(solution)/shard_map/ppermute | solution.py:20
  53.7 2.5 copy-start.1
  53.7 3.9 copy-start.5
  58.1 69.7 %collective-permute-start.2 = (bf16[2,1056,16]{1,2,0:T(8,128)(2,1)S(1)}, bf16[2,1056,16]{1,2,0:T(8,128)(2,1)S(1)}, u32[]{:S(2)}, u32[]{:S(2)}) collective-permute-start(bf16[2,1056,16]{1,2,0:T(8,128)(2,1)S(1)} %copy.10), channel_id=1, source_target_pairs={{0,1},{1,2},{2,3},{3,4},{4,5},{5,6},{6,7},{8,9},{9,10},{10,11},{11... | collective-permute-start | bytes 202760 | tf_op jit(solution)/shard_map/ppermute | solution.py:18
  59.8 68.3 %collective-permute-start.3 = (bf16[2,1056,16]{1,2,0:T(8,128)(2,1)S(1)}, bf16[2,1056,16]{1,2,0:T(8,128)(2,1)S(1)}, u32[]{:S(2)}, u32[]{:S(2)}) collective-permute-start(bf16[2,1056,16]{1,2,0:T(8,128)(2,1)S(1)} %copy.11), channel_id=1, source_target_pairs={{1,0},{2,1},{3,2},{4,3},{5,4},{6,5},{7,6},{9,8},{10,9},{11,10},{12... | collective-permute-start | bytes 202760 | tf_op jit(solution)/shard_map/ppermute | solution.py:20
  290.1 10.5 %copy-start.2 = (f32[1024,512]{1,0:T(8,128)S(1)}, f32[1024,512]{1,0:T(8,128)}, u32[]{:S(2)}) copy-start(f32[1024,512]{1,0:T(8,128)} %param.6) | copy-start | bytes 6291460
  300.6 2.7 copy-start.7
  303.4 138.2 %all-gather.21.cloned.1.call-start = ((), (), s32[]{:S(2)}) async-start(), calls=%async_computation.5 | async-start | bytes 5242880 | tf_op jit(solution)/shard_map/all_gather | solution.py:74
  303.9 194.0 %all-gather.27.cloned.1.call-start = ((), (), s32[]{:S(2)}) async-start(), calls=%async_computation.8 | async-start | bytes 9437184 | tf_op jit(solution)/shard_map/all_gather | solution.py:81
  304.7 276.3 %all-gather.29.cloned.1.call-start = ((), (), s32[]{:S(2)}) async-start(), calls=%async_computation.9 | async-start | bytes 5242880 | tf_op jit(solution)/shard_map/all_gather | solution.py:74
  305.4 331.8 %all-gather.25.cloned.1.call-start = ((), (), s32[]{:S(2)}) async-start(), calls=%async_computation.7 | async-start | bytes 9437184 | tf_op jit(solution)/shard_map/all_gather | solution.py:82
  451.9 2.5 copy-start.8
  454.4 265.0 %all-gather.23.cloned.1.call-start = ((), (), s32[]{:S(2)}) async-start(), calls=%async_computation.6 | async-start | bytes 5242880 | tf_op jit(solution)/shard_map/all_gather | solution.py:75
  457.1 1.3 copy-start.6
  458.4 2.9 collective-permute-start.4
  459.7 5.9 collective-permute-start.5
  467.3 41.0 %collective-permute-start.6 = (bf16[2,1056,16]{1,2,0:T(8,128)(2,1)S(1)}, bf16[2,1056,16]{1,2,0:T(8,128)(2,1)S(1)}, u32[]{:S(2)}, u32[]{:S(2)}) collective-permute-start(bf16[2,1056,16]{1,2,0:T(8,128)(2,1)S(1)} %copy.15), channel_id=1, source_target_pairs={{0,1},{1,2},{2,3},{3,4},{4,5},{5,6},{6,7},{8,9},{9,10},{10,11},{11... | collective-permute-start | bytes 202760 | tf_op jit(solution)/shard_map/ppermute | solution.py:18
  468.8 39.8 %collective-permute-start.7 = (bf16[2,1056,16]{1,2,0:T(8,128)(2,1)S(1)}, bf16[2,1056,16]{1,2,0:T(8,128)(2,1)S(1)}, u32[]{:S(2)}, u32[]{:S(2)}) collective-permute-start(bf16[2,1056,16]{1,2,0:T(8,128)(2,1)S(1)} %copy.16), channel_id=1, source_target_pairs={{1,0},{2,1},{3,2},{4,3},{5,4},{6,5},{7,6},{9,8},{10,9},{11,10},{12... | collective-permute-start | bytes 202760 | tf_op jit(solution)/shard_map/ppermute | solution.py:20
  593.4 126.0 %copy-start.3 = (f32[1024,512]{1,0:T(8,128)S(1)}, f32[1024,512]{1,0:T(8,128)}, u32[]{:S(2)}) copy-start(f32[1024,512]{1,0:T(8,128)} %param.6) | copy-start | bytes 6291460
Sparse Core Ops, SparseCore 0:
  10.1 84.7 all-gather.12
  96.7 54.9 all-gather.10
  153.3 80.7 all-gather.16
  235.8 54.3 all-gather.14
  303.5 55.8 all-gather.18
  360.8 80.7 all-gather.20
  443.4 54.4 all-gather.26
  499.5 81.4 all-gather.28
  582.8 54.3 all-gather.24
  638.6 80.7 all-gather.22
where the time goes:
time: 744 us; the launch traced here: 739 us
  waiting for transfers between devices  432 us (58%)
  other arithmetic  108 us (15%)
  matrix products  87.7 us (12%)
  blocking collectives  47.8 us (6%)
  between operations  41.4 us (6%)
  starting transfers between devices  14.7 us (2%)
    all_gather x2, waiting for transfers between devices, drift(): lax.all_gather(real_low, 'row', axis=0, tiled=True)  109 us
    all_gather x2, waiting for transfers between devices, drift(): lax.all_gather(imag_low, 'col', axis=1, tiled=True)  99.9 us
    all_gather x2, waiting for transfers between devices, drift(): lax.all_gather(real_low, 'col', axis=1, tiled=True)  81.5 us
    all_gather x2, waiting for transfers between devices, drift(): lax.all_gather(imag_low, 'row', axis=0, tiled=True)  71.7 us
    all_gather x1, waiting for transfers between devices, local(): ham_columns = lax.all_gather(hamiltonian, 'row', axis=0, tiled=True)  61.1 us
    add x2, other arithmetic, dissipate(): summed = summed + jnp.where(jump_slot < active, contribution, 0.0)  58.1 us
    psum x1, blocking collectives, local(): lax.psum(diagonal_sum(rho_real, row_first, col_first), ('row', 'col'))  47.8 us
    dot_general x2, matrix products, drift(): left_imag = jnp.dot(strip, pieces[1], preferred_element_type=jnp.float32)  23.2 us
  transfers between devices with their start and end apart: 18, of which 10 were waited for; matrix products, arithmetic and copies ran while one was open for 23% of the time, Pallas kernels for 0%

commit v1 on v0

--- a/solution.py
+++ b/solution.py
@@ -64,7 +64,7 @@
     col_first = lax.axis_index("col") * breadth
     active = active_jumps[0]
     ham_columns = lax.all_gather(hamiltonian, "row", axis=0, tiled=True)
-    start_trace = lax.psum(diagonal_sum(rho_real, row_first, col_first), ("row", "col"))
+    start_trace = lax.psum(lax.psum(diagonal_sum(rho_real, row_first, col_first), "col"), "row")
 
     def drift(real_part, imag_part):
         real_low = real_part.astype(jnp.bfloat16)

time: 744 us -> 744 us (level)
  blocking collectives: 47.8 us -> 29.2 us
  waiting for transfers between devices: 432 us -> 446 us
    psum x1 -> x2, blocking collectives: 47.8 us -> 29.2 us  [the longest x1 14.9 us: local(): lax.psum(diagonal_sum(rho_real, row_first, col_first), 'col')]
    all_gather x1, waiting for transfers between devices: 61.1 us -> 72 us  [local(): ham_columns = lax.all_gather(hamiltonian, 'row', axis=0, tiled=True)]
  transfers between devices with their start and end apart: 18 -> 18, of which waited for: 10 -> 11; matrix products, arithmetic and copies ran while one was open for 23% -> 24% of each run, Pallas kernels for 0% -> 0%
where the time goes in v1:
time: 744 us; the launch traced here: 738 us
  waiting for transfers between devices  446 us (60%)
  other arithmetic  112 us (15%)
  matrix products  87.4 us (12%)
  between operations  41.8 us (6%)
  blocking collectives  29.2 us (4%)
  starting transfers between devices  14.5 us (2%)
    all_gather x2, waiting for transfers between devices, drift(): lax.all_gather(real_low, 'row', axis=0, tiled=True)  109 us
    all_gather x2, waiting for transfers between devices, drift(): lax.all_gather(imag_low, 'col', axis=1, tiled=True)  99.9 us
    all_gather x2, waiting for transfers between devices, drift(): lax.all_gather(real_low, 'col', axis=1, tiled=True)  81.5 us
    all_gather x1, waiting for transfers between devices, local(): ham_columns = lax.all_gather(hamiltonian, 'row', axis=0, tiled=True)  72 us
    all_gather x2, waiting for transfers between devices, drift(): lax.all_gather(imag_low, 'row', axis=0, tiled=True)  71.7 us
    add x2, other arithmetic, dissipate(): summed = summed + jnp.where(jump_slot < active, contribution, 0.0)  58.8 us
    dot_general x2, matrix products, drift(): left_imag = jnp.dot(strip, pieces[1], preferred_element_type=jnp.float32)  22.8 us
    dot_general x2, matrix products, drift(): left_real = jnp.dot(strip, pieces[0], preferred_element_type=jnp.float32)  22.8 us
  transfers between devices with their start and end apart: 18, of which 11 were waited for; matrix products, arithmetic and copies ran while one was open for 24% of the time, Pallas kernels for 0%

profile of v1, /device:TPU:0, one launch (start us, length us, event | category | flops | bytes accessed | tf_op | source)
XLA Modules:
  0.0 737.9 jit_solution(15006518212551161721)
XLA Ops:
  7.2 2.7 convert_element_type.41
  10.0 0.7 all-gather.11.cloned.1.call-update
  10.8 0.7 all-gather.17.cloned.1.call-update
  12.1 2.0 fusion.1
  14.1 1.3 copy-done.3
  15.4 4.9 collective-permute-start
  20.4 1.3 collective-permute-start.1
  21.7 0.7 fusion.69
  32.8 0.6 fusion.62
  33.5 0.7 fusion.64
  34.3 0.7 fusion.58
  35.1 0.6 fusion.60
  35.9 0.6 fusion.54
  36.5 0.7 fusion.56
  37.8 0.6 fusion.52
  38.4 0.7 fusion.50
  39.8 2.9 select_reduce_fusion
  42.7 2.4 add_multiply_fusion.2
  45.1 2.4 add_multiply_fusion.4
  47.5 2.3 add_multiply_fusion.6
  49.8 2.4 add_multiply_fusion.8
  52.2 2.4 broadcast_multiply_fusion
  54.5 2.4 broadcast_multiply_fusion.2
  56.9 2.4 broadcast_multiply_fusion.4
  59.3 14.9 %psum.14 = f32[]{:T(128)} all-reduce(f32[]{:T(128)} %select_reduce_fusion), channel_id=1, replica_groups=mesh['row'=4,'col'=8] {'col'}, use_global_device_ids=true, to_apply=%region_1.2 | all-reduce | flops 1 | bytes 8 | tf_op jit(solution)/shard_map/psum | solution.py:67
  74.3 1.5 pad_maximum_fusion.7
  76.0 1.3 collective-permute-start.2
  77.5 1.3 collective-permute-start.3
  78.8 2.4 broadcast_multiply_fusion.6
  81.3 14.3 %psum.15 = f32[]{:T(128)} all-reduce(f32[]{:T(128)} %psum.14), channel_id=1, replica_groups=mesh['row'=4,'col'=8] {'row'}, use_global_device_ids=true, to_apply=%region_2.3 | all-reduce | flops 1 | bytes 8 | tf_op jit(solution)/shard_map/psum | solution.py:67
  112.9 5.1 maximum_convert_fusion
  118.0 29.2 %select_add_fusion.1 = f32[2,1024,512]{2,1,0:T(8,128)} fusion(f32[2,1056,544]{2,1,0:T(8,128)} %maximum_convert_fusion, s32[]{:T(128)S(6)} %select_n.358, s32[]{:T(128)S(6)} %select_n.359, s32[]{:T(128)S(6)} %select_n.351, s32[]{:T(128)S(6)} %select_n.352, s32[]{:T(128)S(6)} %select_n.344, s32[]{:T(128)S(6)} %select_n.345, s32[]{:T(128)S(6)} %select_n.337, ...), kind=kLoop, calls=%fused_computation.3 | loop fusion | flops 41943040 | bytes 75497544 | tf_op jit(solution)/shard_map/add | solution.py:50
  147.3 3.4 all-gather.11.cloned.1.call-done
  150.7 10.4 %fusion.70 = f32[1024,512]{1,0:T(8,128)} fusion(bf16[1024,4096]{1,0:T(8,128)(2,1)} %all-gather.11.cloned.1.call-done, bf16[4096,512]{1,0:T(8,128)(2,1)} %all-gather.13.cloned.1.call-done), kind=kOutput, calls=%fused_computation.125 | convolution fusion | flops 4294967296 | bytes 14680064 | tf_op jit(solution)/shard_map/dot_general | solution.py:79
  161.1 72.0 %all-gather.17.cloned.1.call-done = bf16[4096,512]{1,0:T(8,128)(2,1)} async-done(((bf16[1024,512]{1,0:T(8,128)(2,1)}), bf16[4096,512]{1,0:T(8,128)(2,1)}) %all-gather.17.cloned.1.call-update) | async-done | bytes 4194320 | tf_op jit(solution)/shard_map/all_gather | solution.py:66
  233.0 56.1 %all-gather.15.cloned.1.call-done = bf16[1024,4096]{1,0:T(8,128)(2,1)} async-done(((bf16[1024,512]{1,0:T(8,128)(2,1)}), bf16[1024,4096]{1,0:T(8,128)(2,1)}) %all-gather.15.cloned.1.call-update) | async-done | bytes 8388624 | tf_op jit(solution)/shard_map/all_gather | solution.py:82
  289.1 10.5 %fusion.13 = f32[1024,512]{1,0:T(8,128)S(1)} fusion(f32[2,1024,512]{2,1,0:T(8,128)} %select_add_fusion.1, f32[1024,512]{1,0:T(8,128)} %fusion.70, bf16[1024,4096]{1,0:T(8,128)(2,1)} %all-gather.15.cloned.1.call-done, bf16[4096,512]{1,0:T(8,128)(2,1)} %all-gather.17.cloned.1.call-done), kind=kOutput, calls=%fused_computation.23 | convolution fusion | flops 4296015872 | bytes 18874368 | tf_op jit(solution)/shard_map/dot_general | solution.py:86
  299.6 2.7 fusion.16
  302.4 0.5 all-gather.21.cloned.1.call-update
  302.9 0.7 all-gather.27.cloned.1.call-update
  303.7 0.7 all-gather.29.cloned.1.call-update
  304.6 53.7 %all-gather.19.cloned.1.call-done = bf16[1024,4096]{1,0:T(8,128)(2,1)} async-done(((bf16[1024,512]{1,0:T(8,128)(2,1)}), bf16[1024,4096]{1,0:T(8,128)(2,1)}) %all-gather.19.cloned.1.call-update) | async-done | bytes 8388624 | tf_op jit(solution)/shard_map/all_gather | solution.py:81
  358.3 10.4 %fusion.71 = f32[1024,512]{1,0:T(8,128)} fusion(bf16[1024,4096]{1,0:T(8,128)(2,1)} %all-gather.19.cloned.1.call-done, bf16[4096,512]{1,0:T(8,128)(2,1)} %all-gather.17.cloned.1.call-done), kind=kOutput, calls=%fused_computation.126 | convolution fusion | flops 4294967296 | bytes 14680064 | tf_op jit(solution)/shard_map/dot_general | solution.py:85
  368.8 71.7 %all-gather.21.cloned.1.call-done = bf16[4096,512]{1,0:T(8,128)(2,1)} async-done(((bf16[1024,512]{1,0:T(8,128)(2,1)}), bf16[4096,512]{1,0:T(8,128)(2,1)}) %all-gather.21.cloned.1.call-update) | async-done | bytes 4194320 | tf_op jit(solution)/shard_map/all_gather | solution.py:74
  440.5 10.3 %fusion.12 = f32[1024,512]{1,0:T(8,128)S(1)} fusion(f32[2,1024,512]{2,1,0:T(8,128)} %select_add_fusion.1, f32[1024,512]{1,0:T(8,128)} %fusion.71, bf16[1024,4096]{1,0:T(8,128)(2,1)} %all-gather.11.cloned.1.call-done, bf16[4096,512]{1,0:T(8,128)(2,1)} %all-gather.21.cloned.1.call-done), kind=kOutput, calls=%fused_computation.21 | convolution fusion | flops 4296015872 | bytes 18874368 | tf_op jit(solution)/shard_map/dot_general | solution.py:78
  450.9 2.5 fusion.15
  453.5 2.6 fusion
  456.1 1.3 copy-done.4
  457.4 1.3 collective-permute-start.4
  458.7 1.3 collective-permute-start.5
  460.3 4.3 collective-permute-done.5
  464.6 1.5 pad_maximum_fusion.4
  466.3 1.3 collective-permute-start.6
  467.8 1.3 collective-permute-start.7
  469.1 27.8 %all-gather.27.cloned.1.call-done = bf16[1024,4096]{1,0:T(8,128)(2,1)} async-done(((bf16[1024,512]{1,0:T(8,128)(2,1)}), bf16[1024,4096]{1,0:T(8,128)(2,1)}) %all-gather.27.cloned.1.call-update) | async-done | bytes 8388624 | tf_op jit(solution)/shard_map/all_gather | solution.py:81
  496.9 10.4 %fusion.73 = f32[1024,512]{1,0:T(8,128)} fusion(bf16[1024,4096]{1,0:T(8,128)(2,1)} %all-gather.27.cloned.1.call-done, bf16[4096,512]{1,0:T(8,128)(2,1)} %all-gather.17.cloned.1.call-done), kind=kOutput, calls=%fused_computation.128 | convolution fusion | flops 4294967296 | bytes 14680064 | tf_op jit(solution)/shard_map/dot_general | solution.py:85
  507.9 5.4 maximum_convert_fusion.1
  513.2 29.5 %select_add_fusion = f32[2,1024,512]{2,1,0:T(8,128)} fusion(f32[2,1056,544]{2,1,0:T(8,128)} %maximum_convert_fusion.1, s32[]{:T(128)S(6)} %select_n.358, s32[]{:T(128)S(6)} %select_n.359, s32[]{:T(128)S(6)} %select_n.351, s32[]{:T(128)S(6)} %select_n.352, s32[]{:T(128)S(6)} %select_n.344, s32[]{:T(128)S(6)} %select_n.345, s32[]{:T(128)S(6)} %select_n.337, ...), kind=kLoop, calls=%fused_computation.2 | loop fusion | flops 41943040 | bytes 75497544 | tf_op jit(solution)/shard_map/add | solution.py:50
  542.8 37.2 %all-gather.29.cloned.1.call-done = bf16[4096,512]{1,0:T(8,128)(2,1)} async-done(((bf16[1024,512]{1,0:T(8,128)(2,1)}), bf16[4096,512]{1,0:T(8,128)(2,1)}) %all-gather.29.cloned.1.call-update) | async-done | bytes 4194320 | tf_op jit(solution)/shard_map/all_gather | solution.py:74
  579.9 12.5 %fusion.6 = f32[1024,512]{1,0:T(8,128)} fusion(f32[1024,512]{1,0:T(8,128)S(1)} %copy-done, f32[1024,512]{1,0:T(8,128)} %copy-done.6, f32[2,1024,512]{2,1,0:T(8,128)} %select_add_fusion, f32[1024,512]{1,0:T(8,128)} %fusion.73, bf16[1024,4096]{1,0:T(8,128)(2,1)} %all-gather.11.cloned.1.call-done, bf16[4096,512]{1,0:T(8,128)(2,1)} %all-gather.29.cloned.1.call-done, ...), kind=kOutput, calls=%fused_computation.13 | convolution fusion | flops 4298113024 | bytes 23068676 | tf_op jit(solution)/shard_map/dot_general | solution.py:78
  592.4 43.8 %all-gather.25.cloned.1.call-done = bf16[1024,4096]{1,0:T(8,128)(2,1)} async-done(((bf16[1024,512]{1,0:T(8,128)(2,1)}), bf16[1024,4096]{1,0:T(8,128)(2,1)}) %all-gather.25.cloned.1.call-update) | async-done | bytes 8388624 | tf_op jit(solution)/shard_map/all_gather | solution.py:82
  636.2 10.5 %fusion.72 = f32[1024,512]{1,0:T(8,128)} fusion(bf16[1024,4096]{1,0:T(8,128)(2,1)} %all-gather.25.cloned.1.call-done, bf16[4096,512]{1,0:T(8,128)(2,1)} %all-gather.17.cloned.1.call-done), kind=kOutput, calls=%fused_computation.127 | convolution fusion | flops 4294967296 | bytes 14680064 | tf_op jit(solution)/shard_map/dot_general | solution.py:86
  646.7 71.7 %all-gather.23.cloned.1.call-done = bf16[4096,512]{1,0:T(8,128)(2,1)} async-done(((bf16[1024,512]{1,0:T(8,128)(2,1)}), bf16[4096,512]{1,0:T(8,128)(2,1)}) %all-gather.23.cloned.1.call-update) | async-done | bytes 4194320 | tf_op jit(solution)/shard_map/all_gather | solution.py:75
  718.4 12.5 %fusion.11 = f32[1024,512]{1,0:T(8,128)} fusion(f32[1024,512]{1,0:T(8,128)S(1)} %copy-done.2, f32[1024,512]{1,0:T(8,128)} %copy-done.5, f32[2,1024,512]{2,1,0:T(8,128)} %select_add_fusion, f32[1024,512]{1,0:T(8,128)} %fusion.72, bf16[1024,4096]{1,0:T(8,128)(2,1)} %all-gather.11.cloned.1.call-done, bf16[4096,512]{1,0:T(8,128)(2,1)} %all-gather.23.cloned.1.call-done, ...), kind=kOutput, calls=%fused_computation.19 | convolution fusion | flops 4298113024 | bytes 23068676 | tf_op jit(solution)/shard_map/dot_general | solution.py:79
  (84 shorter events, 5.5 us)
Async XLA Ops:
  7.2 140.1 %all-gather.13.cloned.1.call-start = ((), (), s32[]{:S(2)}) async-start(), calls=%async_computation.1 | async-start | bytes 5242880 | tf_op jit(solution)/shard_map/all_gather | solution.py:75
  9.9 2.1 copy-start
  10.0 140.7 %all-gather.11.cloned.1.call-start = ((), (), s32[]{:S(2)}) async-start(), calls=%async_computation | async-start | bytes 9437184 | tf_op jit(solution)/shard_map/all_gather | solution.py:72
  10.7 222.3 %all-gather.17.cloned.1.call-start = ((), (), s32[]{:S(2)}) async-start(), calls=%async_computation.3 | async-start | bytes 5242880 | tf_op jit(solution)/shard_map/all_gather | solution.py:66
  11.4 277.7 %all-gather.15.cloned.1.call-start = ((), (), s32[]{:S(2)}) async-start(), calls=%async_computation.2 | async-start | bytes 9437184 | tf_op jit(solution)/shard_map/all_gather | solution.py:82
  12.0 346.3 %all-gather.19.cloned.1.call-start = ((), (), s32[]{:S(2)}) async-start(), calls=%async_computation.4 | async-start | bytes 9437184 | tf_op jit(solution)/shard_map/all_gather | solution.py:81
  12.1 9.6 %copy-start.8 = (s32[8]{0:T(128)S(1)}, s32[8]{0:T(128)}, u32[]{:S(2)}) copy-start(s32[8]{0:T(128)} %param.10) | copy-start | bytes 100
  12.1 20.6 %copy-start.7 = (f32[8,4096]{1,0:T(8,128)S(1)}, f32[8,4096]{1,0:T(8,128)}, u32[]{:S(2)}) copy-start(f32[8,4096]{1,0:T(8,128)} %param.9) | copy-start | bytes 393220
  14.1 1.3 copy-start.3
  15.4 58.9 %collective-permute-start = (bf16[2,16,512]{2,1,0:T(8,128)(2,1)S(1)}, bf16[2,16,512]{2,1,0:T(8,128)(2,1)S(1)}, u32[]{:S(2)}, u32[]{:S(2)}) collective-permute-start(bf16[2,16,512]{2,1,0:T(8,128)(2,1)S(1)} %get-tuple-element.29), channel_id=1, source_target_pairs={{0,8},{8,16},{16,24},{1,9},{9,17},{17,25},{2,10},{10,18},{18,26},{... | collective-permute-start | bytes 98312 | tf_op jit(solution)/shard_map/ppermute | solution.py:18
  20.4 54.0 %collective-permute-start.1 = (bf16[2,16,512]{2,1,0:T(8,128)(2,1)S(1)}, bf16[2,16,512]{2,1,0:T(8,128)(2,1)S(1)}, u32[]{:S(2)}, u32[]{:S(2)}) collective-permute-start(bf16[2,16,512]{2,1,0:T(8,128)(2,1)S(1)} %get-tuple-element.30), channel_id=1, source_target_pairs={{8,0},{16,8},{24,16},{9,1},{17,9},{25,17},{10,2},{18,10},{26,18},{... | collective-permute-start | bytes 98312 | tf_op jit(solution)/shard_map/ppermute | solution.py:20
  76.0 36.3 %collective-permute-start.2 = (bf16[2,1056,16]{1,2,0:T(8,128)(2,1)S(1)}, bf16[2,1056,16]{1,2,0:T(8,128)(2,1)S(1)}, u32[]{:S(2)}, u32[]{:S(2)}) collective-permute-start(bf16[2,1056,16]{1,2,0:T(8,128)(2,1)S(1)} %copy.10), channel_id=1, source_target_pairs={{0,1},{1,2},{2,3},{3,4},{4,5},{5,6},{6,7},{8,9},{9,10},{10,11},{11... | collective-permute-start | bytes 202760 | tf_op jit(solution)/shard_map/ppermute | solution.py:18
  77.5 35.1 %collective-permute-start.3 = (bf16[2,1056,16]{1,2,0:T(8,128)(2,1)S(1)}, bf16[2,1056,16]{1,2,0:T(8,128)(2,1)S(1)}, u32[]{:S(2)}, u32[]{:S(2)}) collective-permute-start(bf16[2,1056,16]{1,2,0:T(8,128)(2,1)S(1)} %copy.11), channel_id=1, source_target_pairs={{1,0},{2,1},{3,2},{4,3},{5,4},{6,5},{7,6},{9,8},{10,9},{11,10},{12... | collective-permute-start | bytes 202760 | tf_op jit(solution)/shard_map/ppermute | solution.py:20
  289.1 10.5 %copy-start.1 = (f32[1024,512]{1,0:T(8,128)S(1)}, f32[1024,512]{1,0:T(8,128)}, u32[]{:S(2)}) copy-start(f32[1024,512]{1,0:T(8,128)} %param.6) | copy-start | bytes 6291460
  299.6 2.7 copy-start.5
  302.3 138.2 %all-gather.21.cloned.1.call-start = ((), (), s32[]{:S(2)}) async-start(), calls=%async_computation.5 | async-start | bytes 5242880 | tf_op jit(solution)/shard_map/all_gather | solution.py:74
  302.9 194.0 %all-gather.27.cloned.1.call-start = ((), (), s32[]{:S(2)}) async-start(), calls=%async_computation.8 | async-start | bytes 9437184 | tf_op jit(solution)/shard_map/all_gather | solution.py:81
  303.7 276.3 %all-gather.29.cloned.1.call-start = ((), (), s32[]{:S(2)}) async-start(), calls=%async_computation.9 | async-start | bytes 5242880 | tf_op jit(solution)/shard_map/all_gather | solution.py:74
  304.4 331.8 %all-gather.25.cloned.1.call-start = ((), (), s32[]{:S(2)}) async-start(), calls=%async_computation.7 | async-start | bytes 9437184 | tf_op jit(solution)/shard_map/all_gather | solution.py:82
  450.9 2.5 copy-start.6
  453.4 264.9 %all-gather.23.cloned.1.call-start = ((), (), s32[]{:S(2)}) async-start(), calls=%async_computation.6 | async-start | bytes 5242880 | tf_op jit(solution)/shard_map/all_gather | solution.py:75
  456.1 1.3 copy-start.4
  457.4 2.9 collective-permute-start.4
  458.7 5.9 collective-permute-start.5
  466.3 41.0 %collective-permute-start.6 = (bf16[2,1056,16]{1,2,0:T(8,128)(2,1)S(1)}, bf16[2,1056,16]{1,2,0:T(8,128)(2,1)S(1)}, u32[]{:S(2)}, u32[]{:S(2)}) collective-permute-start(bf16[2,1056,16]{1,2,0:T(8,128)(2,1)S(1)} %copy.15), channel_id=1, source_target_pairs={{0,1},{1,2},{2,3},{3,4},{4,5},{5,6},{6,7},{8,9},{9,10},{10,11},{11... | collective-permute-start | bytes 202760 | tf_op jit(solution)/shard_map/ppermute | solution.py:18
  467.8 39.8 %collective-permute-start.7 = (bf16[2,1056,16]{1,2,0:T(8,128)(2,1)S(1)}, bf16[2,1056,16]{1,2,0:T(8,128)(2,1)S(1)}, u32[]{:S(2)}, u32[]{:S(2)}) collective-permute-start(bf16[2,1056,16]{1,2,0:T(8,128)(2,1)S(1)} %copy.16), channel_id=1, source_target_pairs={{1,0},{2,1},{3,2},{4,3},{5,4},{6,5},{7,6},{9,8},{10,9},{11,10},{12... | collective-permute-start | bytes 202760 | tf_op jit(solution)/shard_map/ppermute | solution.py:20
  592.4 126.0 %copy-start.2 = (f32[1024,512]{1,0:T(8,128)S(1)}, f32[1024,512]{1,0:T(8,128)}, u32[]{:S(2)}) copy-start(f32[1024,512]{1,0:T(8,128)} %param.6) | copy-start | bytes 6291460
Sparse Core Ops, SparseCore 0:
  10.1 84.2 all-gather.12
  96.3 54.3 all-gather.10
  152.3 80.7 all-gather.16
  234.8 54.3 all-gather.14
  302.4 55.8 all-gather.18
  359.8 80.7 all-gather.20
  442.4 54.4 all-gather.26
  498.5 81.4 all-gather.28
  581.8 54.3 all-gather.24
  637.6 80.7 all-gather.22
